TPU v7x, 512 devices: a whole 4x8x8 slice. The times are simulated.
512 devices in a mesh: batch: 64 (over x, z, y_hi), space: 8 (over y_lo, core).
Axes of the slice: x: 4, y: 8 (y_hi: 2, y_lo: 4; y = y_hi * 4 + y_lo), z: 8, core: 2. Of those that a mesh axis runs over, the one named last changes fastest.
Arguments:
- latents: float32 [64, 32, 64, 4], P('batch', 'space'), may hold values from -16 to 16
- noise_draw: float32 [64, 32, 64, 4], P('batch', 'space'), may hold values from -5 to 5
- timesteps: int32 [64], P('batch'), may hold values from 200 to 799
- inlet_conv: bfloat16 [36, 320], replicated, may hold values from -1 to 1
- time_first: bfloat16 [320, 1280], P(None, 'batch'), may hold values from -0.3125 to 0.3125
- time_first_bias: float32 [1280], replicated, may hold values from -4 to 4
- time_second: bfloat16 [1280, 320], P(None, 'batch'), may hold values from -0.3125 to 0.3125
- time_second_bias: float32 [320], replicated, may hold values from -4 to 4
- conv_first: bfloat16 [2880, 320], P(None, 'batch'), may hold values from -0.109375 to 0.109375
- conv_second: bfloat16 [2880, 320], P(None, 'batch'), may hold values from -0.109375 to 0.109375
- proj_inner: bfloat16 [320, 320], P(None, 'batch'), may hold values from -0.3125 to 0.3125
- query_weight: bfloat16 [320, 320], P(None, 'batch'), may hold values from -30 to 30
- key_weight: bfloat16 [320, 320], P(None, 'batch'), may hold values from -1 to 1
- value_weight: bfloat16 [320, 320], P(None, 'batch'), may hold values from -0.625 to 0.625
- attn_out: bfloat16 [320, 320], P(None, 'batch'), may hold values from -0.625 to 0.625
- proj_outer: bfloat16 [320, 320], P(None, 'batch'), may hold values from -0.3125 to 0.3125
- outlet_conv: bfloat16 [2880, 4], replicated, may hold values from -0.109375 to 0.109375
- first_gain: float32 [320], replicated, may hold values from 0.1 to 1.9
- second_gain: float32 [320], replicated, may hold values from 0.1 to 1.9
- third_gain: float32 [320], replicated, may hold values from 0.1 to 1.9
- final_gain: float32 [320], replicated, may hold values from 0.1 to 1.9
- layer_gain: float32 [320], replicated, may hold values from 0.1 to 1.9
Outputs:
- guidance: float32 [64, 32, 64, 4], P('batch', 'space')
All inputs are finite; a program needn't handle non-finite values.
Results may differ from a plain program's by a relative error of at most 0.029.
Values may be sent and summed in bfloat16 or wider, within the bound.
A program may use at most 64 MiB of HBM per device.

v0:
```python
import math
import jax
import jax.numpy as jnp
from jax import lax
from jax.sharding import PartitionSpec as P

HEADS = 8
HEAD_SIZE = 40
GROUPS = 32
STEPS = 1000
EPS_GROUP = 1e-06
EPS_BLOCK = 1e-05
EPS_LAYER = 1e-05


def laid_out(parts, dim):
    parts = jnp.moveaxis(parts, 0, dim)
    shape = parts.shape
    return parts.reshape(*shape[:dim], shape[dim] * shape[dim + 1], *shape[dim + 2 :])


def from_everyone(shard, axis):
    length = lax.axis_size(axis)
    return lax.all_to_all(
        jnp.broadcast_to(shard[None], (length, *shard.shape)), axis, 0, 0, tiled=True
    )


def collect(shard, axis, dim):
    return laid_out(from_everyone(shard, axis), dim)


def extended(cells, sides, width):
    for axis, dim in sides:
        count = lax.axis_size(axis)
        ends = count - 1
        head = lax.slice_in_dim(cells, 0, width, axis=dim)
        tail = lax.slice_in_dim(cells, cells.shape[dim] - width, cells.shape[dim], axis=dim)
        cells = jnp.concatenate(
            [
                lax.ppermute(tail, axis, [(i, (i + 1) % count) for i in range(ends)]),
                cells,
                lax.ppermute(head, axis, [((i + 1) % count, i) for i in range(ends)]),
            ],
            axis=dim,
        )
    return cells


def of_everyone(shard, axis):
    everything = from_everyone(shard, axis)
    return jnp.sum(everything, axis=0)


def packed_total(arrays, axis):
    vector, at, gathered = (jnp.concatenate([a.reshape(-1) for a in arrays]), 0, [])
    running = of_everyone(vector, axis)
    for a in arrays:
        gathered.append(running[at : at + a.size].reshape(a.shape))
        at += a.size
    return tuple(gathered)


def in_one_piece(arrays, axis, dim, along):
    widths = [a.shape[along] for a in arrays]
    both = jnp.concatenate(arrays, axis=along)
    filled = lax.all_gather(both, axis, axis=dim, tiled=True)
    return tuple(jnp.split(filled, [sum(widths[:k]) for k in range(1, len(widths))], axis=along))


def turned_gather(arrays, axis, dims):
    turned = [jnp.moveaxis(a, dim, 0) for a, dim in zip(arrays, dims)]
    widths = [t[0].size for t in turned]
    both = jnp.concatenate([t.reshape(-1, w) for t, w in zip(turned, widths)], axis=1)
    filled = lax.all_gather(both, axis, axis=0, tiled=True)
    parts = jnp.split(filled, [sum(widths[:k]) for k in range(1, len(widths))], axis=1)
    return tuple(
        (
            jnp.moveaxis(b.reshape(-1, *t.shape[1:]), 0, dim)
            for b, t, dim in zip(parts, turned, dims)
        )
    )


def plan():
    fraction = jnp.arange(STEPS, dtype=jnp.float32) / (STEPS - 1)
    beta_root = math.sqrt(0.00085) + fraction * (math.sqrt(0.012) - math.sqrt(0.00085))
    return jnp.cumprod(1.0 - beta_root * beta_root)


def lookup(timesteps):
    plan_tab = plan()
    matches = jnp.arange(STEPS, dtype=jnp.int32)[None, :] == timesteps[:, None]
    return jnp.sum(jnp.where(matches, plan_tab[None, :], 0.0), axis=1)


def waveform_of(timesteps, halfway):
    frequency = jnp.exp(-math.log(10000.0) * jnp.arange(halfway, dtype=jnp.float32) / halfway)
    angles = timesteps.astype(jnp.float32)[:, None] * frequency[None, :]
    return jnp.concatenate([jnp.cos(angles), jnp.sin(angles)], axis=1).astype(jnp.bfloat16)


def embed_sharded(timesteps, first, first_bias, second, second_bias):
    all_steps = collect(timesteps, "batch", 0)
    position = lax.axis_index("batch")
    width_one = first.shape[1]
    width_two = second.shape[1]
    waveform = waveform_of(all_steps, first.shape[0] // 2)
    bias_one = lax.dynamic_slice_in_dim(first_bias, position * width_one, width_one, 0)
    inner = jax.nn.silu(jnp.dot(waveform, first, preferred_element_type=jnp.float32) + bias_one)
    hidden = jax.nn.silu(inner).astype(jnp.bfloat16)
    hidden_all = collect(hidden, "batch", 1)
    bias_two = lax.dynamic_slice_in_dim(second_bias, position * width_two, width_two, 0)
    columns = jnp.dot(hidden_all, second, preferred_element_type=jnp.float32) + bias_two
    return lax.all_to_all(columns, "batch", split_axis=0, concat_axis=1, tiled=True)


def convolve(padded, kernel):
    height = padded.shape[1] - 2
    breadth = padded.shape[2] - 2
    width_in = padded.shape[3]
    result = None
    for offset in range(9):
        row_off, col_off = (offset // 3, offset % 3)
        window = padded[:, row_off : row_off + height, col_off : col_off + breadth, :]
        partial_sum = jnp.einsum(
            "bhwc,cd->bhwd",
            window,
            kernel[offset * width_in : (offset + 1) * width_in],
            preferred_element_type=jnp.float32,
        )
        result = partial_sum if result is None else result + partial_sum
    return result


def with_rims(field):
    padded = extended(field, (("space", 1),), 1)
    return jnp.pad(padded, ((0, 0), (0, 0), (1, 1), (0, 0)))


def with_latent_rims(field):
    padded = extended(field, (("space", 1),), 1)
    return jnp.pad(padded, ((0, 0), (0, 0), (1, 1), (0, 0)))


def group_norm(field, gain_vec, epsilon):
    view_n, height, breadth, chan_n = field.shape
    grouped = field.reshape(view_n, height, breadth, GROUPS, chan_n // GROUPS)
    sums_local = jnp.sum(grouped, axis=(1, 2, 4))
    squares_local = jnp.sum(grouped * grouped, axis=(1, 2, 4))
    sums_all, squares_all = packed_total((sums_local, squares_local), "space")
    number = height * lax.axis_size("space") * breadth * (chan_n // GROUPS)
    means = sums_all / number
    squares = squares_all / number
    factor = lax.rsqrt(squares - means * means + epsilon)
    normal_f = (grouped - means[:, None, None, :, None]) * factor[:, None, None, :, None]
    return normal_f.reshape(view_n, height, breadth, chan_n) * gain_vec


def layer_norm(field, gain_vec):
    means = jnp.mean(field, axis=-1, keepdims=True)
    centred = field - means
    spread = jnp.mean(centred * centred, axis=-1, keepdims=True)
    return centred * lax.rsqrt(spread + EPS_LAYER) * gain_vec


def keys_everywhere(queries, key_rows, value_rows):
    view_n, token_n, chan_n = queries.shape
    factor = 1.0 / math.sqrt(HEAD_SIZE)
    query_heads = queries.reshape(view_n, token_n, HEADS, HEAD_SIZE)
    row_max = jnp.full((view_n, HEADS, token_n), -jnp.inf, jnp.float32)
    row_sum = jnp.zeros((view_n, HEADS, token_n), jnp.float32)
    accum = jnp.zeros((view_n, HEADS, token_n, HEAD_SIZE), jnp.float32)
    key_part, value_part = in_one_piece((key_rows, value_rows), "space", 1, 0)
    length = key_part.shape[1]
    block_n = min(512, length)
    for offset in range(0, length, block_n):
        key_blk = key_part[:, offset : offset + block_n]
        value_blk = value_part[:, offset : offset + block_n]
        rows_here = key_blk.shape[1]
        key_blk = key_blk.reshape(view_n, rows_here, HEADS, HEAD_SIZE)
        value_blk = value_blk.reshape(view_n, rows_here, HEADS, HEAD_SIZE)
        scores = (
            jnp.einsum("bqhd,bkhd->bhqk", query_heads, key_blk, preferred_element_type=jnp.float32)
            * factor
        )
        new_max = jnp.maximum(row_max, jnp.max(scores, axis=-1))
        shrink = jnp.exp(row_max - new_max)
        weights = jnp.exp(scores - new_max[..., None])
        row_sum = row_sum * shrink + jnp.sum(weights, axis=-1)
        accum = accum * shrink[..., None] + jnp.einsum(
            "bhqk,bkhd->bhqd",
            weights.astype(jnp.bfloat16),
            value_blk,
            preferred_element_type=jnp.float32,
        )
        row_max = new_max
    row_max, row_sum, accum = (row_max, row_sum, accum)
    result = accum / row_sum[..., None]
    return result.transpose(0, 2, 1, 3).reshape(view_n, token_n, chan_n).astype(jnp.bfloat16)


def project(field, matrix):
    return jnp.einsum("btc,cd->btd", field, matrix, preferred_element_type=jnp.float32)


def body(
    latents,
    noise_draw,
    timesteps,
    inlet_conv,
    time_first,
    time_first_bias,
    time_second,
    time_second_bias,
    conv_first,
    conv_second,
    proj_inner,
    query_weight,
    key_weight,
    value_weight,
    attn_out,
    proj_outer,
    outlet_conv,
    first_gain,
    second_gain,
    third_gain,
    final_gain,
    layer_gain,
):
    gathered = turned_gather(
        (
            conv_first,
            conv_second,
            proj_inner,
            query_weight,
            key_weight,
            value_weight,
            attn_out,
            proj_outer,
        ),
        "batch",
        (1, 1, 1, 1, 1, 1, 1, 1),
    )
    conv_one, conv_two, inner_w, query_w, key_w, value_w, output_w, outer_w = gathered
    embedded = embed_sharded(timesteps, time_first, time_first_bias, time_second, time_second_bias)
    alpha_bar = lookup(timesteps)[:, None, None, None]
    noisy = (jnp.sqrt(alpha_bar) * latents + jnp.sqrt(1.0 - alpha_bar) * noise_draw).astype(
        jnp.bfloat16
    )
    opening = convolve(with_latent_rims(noisy), inlet_conv).astype(jnp.bfloat16)
    active = jax.nn.silu(group_norm(opening.astype(jnp.float32), first_gain, EPS_BLOCK)).astype(
        jnp.bfloat16
    )
    middle = (convolve(with_rims(active), conv_one) + embedded[:, None, None, :]).astype(
        jnp.bfloat16
    )
    active = jax.nn.silu(group_norm(middle.astype(jnp.float32), second_gain, EPS_BLOCK)).astype(
        jnp.bfloat16
    )
    block_one = (opening.astype(jnp.float32) + convolve(with_rims(active), conv_two)).astype(
        jnp.bfloat16
    )
    normed = group_norm(block_one.astype(jnp.float32), third_gain, EPS_GROUP).astype(jnp.bfloat16)
    view_n, height, breadth, chan_n = normed.shape
    flattened = normed.reshape(view_n, height * breadth, chan_n)
    projected = project(flattened, inner_w)
    tokens_in = layer_norm(projected, layer_gain).astype(jnp.bfloat16)
    queries = project(tokens_in, query_w).astype(jnp.bfloat16)
    key_rows = project(tokens_in, key_w).astype(jnp.bfloat16)
    value_rows = project(tokens_in, value_w).astype(jnp.bfloat16)
    attended = keys_everywhere(queries, key_rows, value_rows)
    mixture = (project(attended, output_w) + projected).astype(jnp.bfloat16)
    outer = project(mixture, outer_w).reshape(view_n, height, breadth, chan_n)
    block_two = (block_one.astype(jnp.float32) + outer).astype(jnp.bfloat16)
    active = jax.nn.silu(group_norm(block_two.astype(jnp.float32), final_gain, EPS_BLOCK)).astype(
        jnp.bfloat16
    )
    predicted = convolve(with_rims(active), outlet_conv)
    return (1.0 - alpha_bar) * (predicted - noise_draw)


def solution(mesh):
    in_specs = (
        P("batch", "space", None, None),
        P("batch", "space", None, None),
        P("batch"),
        P(),
        P(None, "batch"),
        P(),
        P(None, "batch"),
        P(),
        P(None, "batch"),
        P(None, "batch"),
        P(None, "batch"),
        P(None, "batch"),
        P(None, "batch"),
        P(None, "batch"),
        P(None, "batch"),
        P(None, "batch"),
        P(),
        P(),
        P(),
        P(),
        P(),
        P(),
    )
    out_specs = P("batch", "space", None, None)
    return jax.shard_map(body, mesh=mesh, in_specs=in_specs, out_specs=out_specs, check_vma=False)
```

profile of v0, /device:TPU:1, one launch (start us, length us, event | category | flops | bytes accessed | tf_op | source)
XLA Modules:
  0.0 351.4 jit_solution(13570895085451096625)
XLA Ops:
  12.2 4.6 %collective-permute-start = (bf16[1,1,64,4]{2,3,1,0:T(4,128)(2,1)S(1)}, bf16[1,1,64,4]{2,3,1,0:T(4,128)(2,1)S(1)}, u32[]{:S(2)}, u32[]{:S(2)}) collective-permute-start(bf16[1,1,64,4]{2,3,1,0:T(4,128)(2,1)S(1)} %get-tuple-element.37), channel_id=1, source_target_pairs={{0,1},{1,2},{2,3},{3,4},{4,5},{5,6},{6,7},{8,9},{9,10},{10,11},{11... | collective-permute-start | bytes 1544 | tf_op jit(solution)/shard_map/ppermute | solution.py:41
  16.8 5.5 %collective-permute-start.1 = (bf16[1,1,64,4]{2,3,1,0:T(4,128)(2,1)S(1)}, bf16[1,1,64,4]{2,3,1,0:T(4,128)(2,1)S(1)}, u32[]{:S(2)}, u32[]{:S(2)}) collective-permute-start(bf16[1,1,64,4]{2,3,1,0:T(4,128)(2,1)S(1)} %get-tuple-element.38), channel_id=1, source_target_pairs={{1,0},{2,1},{3,2},{4,3},{5,4},{6,5},{7,6},{9,8},{10,9},{11,10},{12... | collective-permute-start | bytes 1544 | tf_op jit(solution)/shard_map/ppermute | solution.py:43
  22.8 14.3 %all-to-all-start.1 = ((s32[64,1,1]{2,1,0:T(1,128)}), s32[64,1,1]{2,1,0:T(1,128)S(1)}, u32[]{:S(2)}, u32[]{:S(2)}) async-start(s32[64,1,1]{2,1,0:T(1,128)} %broadcast_in_dim.22), calls=%async_computation.1 | async-start | bytes 65536 | tf_op jit(solution)/shard_map/all_to_all | solution.py:24
  38.7 11.6 %all-to-all-done.1 = s32[64,1,1]{2,1,0:T(1,128)S(1)} async-done(((s32[64,1,1]{2,1,0:T(1,128)}), s32[64,1,1]{2,1,0:T(1,128)S(1)}, u32[]{:S(2)}, u32[]{:S(2)}) %all-to-all-start.1) | async-done | bytes 288 | tf_op jit(solution)/shard_map/all_to_all | solution.py:24
  60.2 5.1 %all-to-all-start = ((f32[8,1,64]{2,1,0:T(1,128)}), f32[8,1,64]{2,1,0:T(1,128)S(1)}, u32[]{:S(2)}, u32[]{:S(2)}) async-start(f32[8,1,64]{2,1,0:T(1,128)} %broadcast_in_dim.21), calls=%async_computation | async-start | bytes 8192 | tf_op jit(solution)/shard_map/all_to_all | solution.py:24
  66.2 3.9 %all-to-all-done = f32[8,1,64]{2,1,0:T(1,128)S(1)} async-done(((f32[8,1,64]{2,1,0:T(1,128)}), f32[8,1,64]{2,1,0:T(1,128)S(1)}, u32[]{:S(2)}, u32[]{:S(2)}) %all-to-all-start) | async-done | bytes 2080 | tf_op jit(solution)/shard_map/all_to_all | solution.py:24
  70.1 4.6 %all-to-all-start.2 = ((bf16[64,2,640]{2,1,0:T(2,128)(2,1)}), bf16[64,2,640]{2,1,0:T(2,128)(2,1)S(1)}, u32[]{:S(2)}, u32[]{:S(2)}) async-start(bf16[64,2,640]{2,1,0:T(2,128)(2,1)} %reshape.912), calls=%async_computation.2 | async-start | bytes 327680 | tf_op jit(solution)/shard_map/all_to_all | solution.py:24
  75.3 2.8 collective-permute-start.2
  80.0 9.5 %all-to-all-done.2 = bf16[64,2,640]{2,1,0:T(2,128)(2,1)S(1)} async-done(((bf16[64,2,640]{2,1,0:T(2,128)(2,1)}), bf16[64,2,640]{2,1,0:T(2,128)(2,1)S(1)}, u32[]{:S(2)}, u32[]{:S(2)}) %all-to-all-start.2) | async-done | bytes 163872 | tf_op jit(solution)/shard_map/all_to_all | solution.py:24
  91.0 6.6 %all-to-all-start.3 = ((f32[64,1,5]{2,1,0:T(1,128)}), f32[64,1,5]{2,1,0:T(1,128)S(1)}, u32[]{:S(2)}, u32[]{:S(2)}) async-start(f32[64,1,5]{2,1,0:T(1,128)} %copy.45), calls=%async_computation.3 | async-start | bytes 65536 | tf_op jit(solution)/shard_map/all_to_all | solution.py:115
  97.8 12.9 %all-to-all-done.3 = f32[64,1,5]{2,1,0:T(1,128)S(1)} async-done(((f32[64,1,5]{2,1,0:T(1,128)}), f32[64,1,5]{2,1,0:T(1,128)S(1)}, u32[]{:S(2)}, u32[]{:S(2)}) %all-to-all-start.3) | async-done | bytes 1312 | tf_op jit(solution)/shard_map/all_to_all | solution.py:115
  112.1 89.3 %all-gather.6.cloned.1.call-done = bf16[64,5,7680]{2,1,0:T(8,128)(2,1)} async-done(((bf16[1,5,7680]{2,1,0:T(8,128)(2,1)}), bf16[64,5,7680]{2,1,0:T(8,128)(2,1)}) %all-gather.6.cloned.1.call-update) | async-done | bytes 4915216 | tf_op jit(solution)/shard_map/all_gather | solution.py:75
  201.4 8.5 %reshape.863 = bf16[320,7680]{1,0:T(8,128)(2,1)} reshape(bf16[64,5,7680]{2,1,0:T(8,128)(2,1)} %all-gather.6.cloned.1.call-done) | data formatting | bytes 9830400
  209.9 4.3 %fusion.187 = (bf16[320,2880]{1,0:T(8,128)(2,1)}, bf16[320,2880]{1,0:T(8,128)(2,1)S(1)}) fusion(bf16[320,7680]{1,0:T(8,128)(2,1)} %reshape.863), kind=kLoop, calls=%fused_computation.299 | loop fusion | bytes 7372800 | tf_op jit(solution)/shard_map/split | solution.py:76
  214.2 4.0 %copy.51 = bf16[320,2880]{0,1:T(8,128)(2,1)} copy(bf16[320,2880]{1,0:T(8,128)(2,1)} %get-tuple-element.20) | data formatting | bytes 3686400
  225.2 13.7 %all_to_all.48 = f32[8,1,64]{2,1,0:T(1,128)S(1)} all-to-all(f32[8,1,64]{2,1,0:T(1,128)S(1)} %broadcast_in_dim.24), channel_id=1, replica_groups=mesh['batch'=64,'space'=8] {'space'}, dimensions={0} | all-to-all | bytes 4096 | tf_op jit(solution)/shard_map/all_to_all | solution.py:24
  239.5 2.8 collective-permute-start.4
  244.4 2.6 copy.52
  254.7 7.6 %all_to_all.49 = f32[8,1,64]{2,1,0:T(1,128)S(1)} all-to-all(f32[8,1,64]{2,1,0:T(1,128)S(1)} %broadcast_in_dim.26), channel_id=1, replica_groups=mesh['batch'=64,'space'=8] {'space'}, dimensions={0} | all-to-all | bytes 4096 | tf_op jit(solution)/shard_map/all_to_all | solution.py:24
  268.7 38.4 %all-gather.4.cloned.1.call-done = bf16[2,2048,320]{1,2,0:T(8,128)(2,1)} async-done(((bf16[2,256,320]{1,2,0:T(8,128)(2,1)}), bf16[2,2048,320]{1,2,0:T(8,128)(2,1)}) %all-gather.4.cloned.1.call-update) | async-done | bytes 2621456 | tf_op jit(solution)/shard_map/all_gather | solution.py:67
  314.5 2.2 fusion.2
  324.7 8.2 %all_to_all.50 = f32[8,1,64]{2,1,0:T(1,128)S(1)} all-to-all(f32[8,1,64]{2,1,0:T(1,128)S(1)} %broadcast_in_dim.28), channel_id=1, replica_groups=mesh['batch'=64,'space'=8] {'space'}, dimensions={0} | all-to-all | bytes 4096 | tf_op jit(solution)/shard_map/all_to_all | solution.py:24
  333.5 2.8 collective-permute-start.6
  338.3 3.5 collective-permute-done.7
  (183 shorter events, 66.2 us)
Async XLA Ops:
  6.5 83.5 %copy-start = (bf16[1280,5]{0,1:T(8,128)(2,1)S(1)}, bf16[1280,5]{0,1:T(8,128)(2,1)}, u32[]{:S(2)}) copy-start(bf16[1280,5]{0,1:T(8,128)(2,1)} %param.28) | copy-start | bytes 38404
  6.5 51.6 %copy-start.3 = (bf16[36,320]{1,0:T(8,128)(2,1)S(1)}, bf16[36,320]{1,0:T(8,128)(2,1)}, u32[]{:S(2)}) copy-start(bf16[36,320]{1,0:T(8,128)(2,1)} %param.25) | copy-start | bytes 69124
  6.5 194.9 %all-gather.6.cloned.1.call-start = ((), (), s32[]{:S(2)}) async-start(), calls=%async_computation.8 | async-start | bytes 7987200 | tf_op jit(solution)/shard_map/all_gather | solution.py:75
  12.2 40.0 %collective-permute-start = (bf16[1,1,64,4]{2,3,1,0:T(4,128)(2,1)S(1)}, bf16[1,1,64,4]{2,3,1,0:T(4,128)(2,1)S(1)}, u32[]{:S(2)}, u32[]{:S(2)}) collective-permute-start(bf16[1,1,64,4]{2,3,1,0:T(4,128)(2,1)S(1)} %get-tuple-element.37), channel_id=1, source_target_pairs={{0,1},{1,2},{2,3},{3,4},{4,5},{5,6},{6,7},{8,9},{9,10},{10,11},{11... | collective-permute-start | bytes 1544 | tf_op jit(solution)/shard_map/ppermute | solution.py:41
  16.8 35.4 %collective-permute-start.1 = (bf16[1,1,64,4]{2,3,1,0:T(4,128)(2,1)S(1)}, bf16[1,1,64,4]{2,3,1,0:T(4,128)(2,1)S(1)}, u32[]{:S(2)}, u32[]{:S(2)}) collective-permute-start(bf16[1,1,64,4]{2,3,1,0:T(4,128)(2,1)S(1)} %get-tuple-element.38), channel_id=1, source_target_pairs={{1,0},{2,1},{3,2},{4,3},{5,4},{6,5},{7,6},{9,8},{10,9},{11,10},{12... | collective-permute-start | bytes 1544 | tf_op jit(solution)/shard_map/ppermute | solution.py:43
  22.8 27.5 %all-to-all-start.1 = ((s32[64,1,1]{2,1,0:T(1,128)}), s32[64,1,1]{2,1,0:T(1,128)S(1)}, u32[]{:S(2)}, u32[]{:S(2)}) async-start(s32[64,1,1]{2,1,0:T(1,128)} %broadcast_in_dim.22), calls=%async_computation.1 | async-start | bytes 65536 | tf_op jit(solution)/shard_map/all_to_all | solution.py:24
  51.2 24.0 %copy-start.5 = (f32[320]{0:T(512)S(1)}, f32[320]{0:T(512)}, u32[]{:S(2)}) copy-start(f32[320]{0:T(512)} %param.39) | copy-start | bytes 3844
  60.2 9.9 %all-to-all-start = ((f32[8,1,64]{2,1,0:T(1,128)}), f32[8,1,64]{2,1,0:T(1,128)S(1)}, u32[]{:S(2)}, u32[]{:S(2)}) async-start(f32[8,1,64]{2,1,0:T(1,128)} %broadcast_in_dim.21), calls=%async_computation | async-start | bytes 8192 | tf_op jit(solution)/shard_map/all_to_all | solution.py:24
  70.1 19.5 %all-to-all-start.2 = ((bf16[64,2,640]{2,1,0:T(2,128)(2,1)}), bf16[64,2,640]{2,1,0:T(2,128)(2,1)S(1)}, u32[]{:S(2)}, u32[]{:S(2)}) async-start(bf16[64,2,640]{2,1,0:T(2,128)(2,1)} %reshape.912), calls=%async_computation.2 | async-start | bytes 327680 | tf_op jit(solution)/shard_map/all_to_all | solution.py:24
  75.3 22.3 %collective-permute-start.2 = (bf16[1,1,64,320]{3,2,1,0:T(8,128)(2,1)S(1)}, bf16[1,1,64,320]{3,2,1,0:T(8,128)(2,1)S(1)}, u32[]{:S(2)}, u32[]{:S(2)}) collective-permute-start(bf16[1,1,64,320]{3,2,1,0:T(8,128)(2,1)S(1)} %get-tuple-element.34), channel_id=1, source_target_pairs={{0,1},{1,2},{2,3},{3,4},{4,5},{5,6},{6,7},{8,9},{9,10},{10,11},{11... | collective-permute-start | bytes 122888 | tf_op jit(solution)/shard_map/ppermute | solution.py:41
  78.1 19.6 %collective-permute-start.3 = (bf16[1,1,64,320]{3,2,1,0:T(8,128)(2,1)S(1)}, bf16[1,1,64,320]{3,2,1,0:T(8,128)(2,1)S(1)}, u32[]{:S(2)}, u32[]{:S(2)}) collective-permute-start(bf16[1,1,64,320]{3,2,1,0:T(8,128)(2,1)S(1)} %get-tuple-element.35), channel_id=1, source_target_pairs={{1,0},{2,1},{3,2},{4,3},{5,4},{6,5},{7,6},{9,8},{10,9},{11,10},{12... | collective-permute-start | bytes 122888 | tf_op jit(solution)/shard_map/ppermute | solution.py:43
  91.0 19.8 %all-to-all-start.3 = ((f32[64,1,5]{2,1,0:T(1,128)}), f32[64,1,5]{2,1,0:T(1,128)S(1)}, u32[]{:S(2)}, u32[]{:S(2)}) async-start(f32[64,1,5]{2,1,0:T(1,128)} %copy.45), calls=%async_computation.3 | async-start | bytes 65536 | tf_op jit(solution)/shard_map/all_to_all | solution.py:115
  97.6 209.5 %all-gather.4.cloned.1.call-start = ((), (), s32[]{:S(2)}) async-start(), calls=%async_computation.7 | async-start | bytes 2949120 | tf_op jit(solution)/shard_map/all_gather | solution.py:67
  223.2 16.1 %copy-start.6 = (f32[320]{0:T(512)S(1)}, f32[320]{0:T(512)}, u32[]{:S(2)}) copy-start(f32[320]{0:T(512)} %param.40) | copy-start | bytes 3844
  239.5 7.5 %collective-permute-start.4 = (bf16[1,1,64,320]{3,2,1,0:T(8,128)(2,1)S(1)}, bf16[1,1,64,320]{3,2,1,0:T(8,128)(2,1)S(1)}, u32[]{:S(2)}, u32[]{:S(2)}) collective-permute-start(bf16[1,1,64,320]{3,2,1,0:T(8,128)(2,1)S(1)} %get-tuple-element.32), channel_id=1, source_target_pairs={{0,1},{1,2},{2,3},{3,4},{4,5},{5,6},{6,7},{8,9},{9,10},{10,11},{11... | collective-permute-start | bytes 122888 | tf_op jit(solution)/shard_map/ppermute | solution.py:41
  242.3 5.4 %collective-permute-start.5 = (bf16[1,1,64,320]{3,2,1,0:T(8,128)(2,1)S(1)}, bf16[1,1,64,320]{3,2,1,0:T(8,128)(2,1)S(1)}, u32[]{:S(2)}, u32[]{:S(2)}) collective-permute-start(bf16[1,1,64,320]{3,2,1,0:T(8,128)(2,1)S(1)} %get-tuple-element.33), channel_id=1, source_target_pairs={{1,0},{2,1},{3,2},{4,3},{5,4},{6,5},{7,6},{9,8},{10,9},{11,10},{12... | collective-permute-start | bytes 122888 | tf_op jit(solution)/shard_map/ppermute | solution.py:43
  247.0 5.6 %copy-start.1 = (bf16[320,2880]{0,1:T(8,128)(2,1)S(1)}, bf16[320,2880]{0,1:T(8,128)(2,1)}, u32[]{:S(2)}) copy-start(bf16[320,2880]{0,1:T(8,128)(2,1)} %copy.52) | copy-start | bytes 5529604
  252.6 10.0 %copy-start.7 = (f32[320]{0:T(512)S(1)}, f32[320]{0:T(512)}, u32[]{:S(2)}) copy-start(f32[320]{0:T(512)} %param.41) | copy-start | bytes 3844
  252.9 11.2 %copy-start.8 = (f32[320]{0:T(512)S(1)}, f32[320]{0:T(512)}, u32[]{:S(2)}) copy-start(f32[320]{0:T(512)} %param.43) | copy-start | bytes 3844
  320.4 13.0 %copy-start.9 = (f32[320]{0:T(512)S(1)}, f32[320]{0:T(512)}, u32[]{:S(2)}) copy-start(f32[320]{0:T(512)} %param.42) | copy-start | bytes 3844
  320.4 21.4 %copy-start.10 = (bf16[2880,4]{0,1:T(4,128)(2,1)S(1)}, bf16[2880,4]{0,1:T(4,128)(2,1)}, u32[]{:S(2)}) copy-start(bf16[2880,4]{0,1:T(4,128)(2,1)} %param.38) | copy-start | bytes 69124
  321.4 22.2 %copy-start.4 = (f32[1,4,64,4]{2,3,1,0:T(4,128)S(1)}, f32[1,4,64,4]{2,3,1,0:T(4,128)}, u32[]{:S(2)}) copy-start(f32[1,4,64,4]{2,3,1,0:T(4,128)} %param.23) | copy-start | bytes 12292
  333.5 4.7 %collective-permute-start.6 = (bf16[1,1,64,320]{3,2,1,0:T(8,128)(2,1)S(1)}, bf16[1,1,64,320]{3,2,1,0:T(8,128)(2,1)S(1)}, u32[]{:S(2)}, u32[]{:S(2)}) collective-permute-start(bf16[1,1,64,320]{3,2,1,0:T(8,128)(2,1)S(1)} %get-tuple-element.30), channel_id=1, source_target_pairs={{0,1},{1,2},{2,3},{3,4},{4,5},{5,6},{6,7},{8,9},{9,10},{10,11},{11... | collective-permute-start | bytes 122888 | tf_op jit(solution)/shard_map/ppermute | solution.py:41
  336.3 5.4 %collective-permute-start.7 = (bf16[1,1,64,320]{3,2,1,0:T(8,128)(2,1)S(1)}, bf16[1,1,64,320]{3,2,1,0:T(8,128)(2,1)S(1)}, u32[]{:S(2)}, u32[]{:S(2)}) collective-permute-start(bf16[1,1,64,320]{3,2,1,0:T(8,128)(2,1)S(1)} %get-tuple-element.31), channel_id=1, source_target_pairs={{1,0},{2,1},{3,2},{4,3},{5,4},{6,5},{7,6},{9,8},{10,9},{11,10},{12... | collective-permute-start | bytes 122888 | tf_op jit(solution)/shard_map/ppermute | solution.py:43
  (1 other events, 5.0 us)
Sparse Core Ops, SparseCore 0:
  11.9 189.5 all-gather.5
  267.6 39.4 all-gather.3
where the time goes:
time: 353 us; the launch traced here: 351 us
  waiting for transfers between devices  170 us (48%)
  starting transfers between devices  55 us (16%)
  matrix products  38.7 us (11%)
  local copies, waits for them, and re-layouts  31.1 us (9%)
  blocking collectives  29.4 us (8%)
  between operations  16.2 us (5%)
  other arithmetic  11.2 us (3%)
    all_gather x1, waiting for transfers between devices, turned_gather(): filled = lax.all_gather(both, axis, axis=0, tiled=True)  89.3 us
    all_gather x1, waiting for transfers between devices, in_one_piece(): filled = lax.all_gather(both, axis, axis=dim, tiled=True)  38.4 us
    all_to_all x3, blocking collectives, from_everyone(): lax.all_to_all(jnp.broadcast_to(shard[None], (length, *shard.shape)), axi...  29.4 us
    all_to_all x3, waiting for transfers between devices, from_everyone(): lax.all_to_all(jnp.broadcast_to(shard[None], (length, *shard.shape)), axi...  25 us
    all_to_all x3, starting transfers between devices, from_everyone(): lax.all_to_all(jnp.broadcast_to(shard[None], (length, *shard.shape)), axi...  24 us
    dot_general x36, matrix products, convolve(): jnp.einsum('bhwc,cd->bhwd', window, kernel[offset * width_in:(offset + 1)...  22.1 us
    unnamed x28, local copies, waits for them, and re-layouts  16.4 us
    ppermute x4, starting transfers between devices, extended(): lax.ppermute(tail, axis, [(i, (i + 1) % count) for i in range(ends)])  12.9 us
  transfers between devices with their start and end apart: 14, of which 8 were waited for; matrix products, arithmetic and copies ran while one was open for 6% of the time, Pallas kernels for 0%

commit v1 on v0

--- a/solution.py
+++ b/solution.py
@@ -72,7 +72,10 @@
     turned = [jnp.moveaxis(a, dim, 0) for a, dim in zip(arrays, dims)]
     widths = [t[0].size for t in turned]
     both = jnp.concatenate([t.reshape(-1, w) for t, w in zip(turned, widths)], axis=1)
-    filled = lax.all_gather(both, axis, axis=0, tiled=True)
+    n_dev = lax.axis_size(axis)
+    blocks = jnp.stack([both for _ in range(n_dev)])
+    blocks = lax.all_to_all(blocks, axis, split_axis=0, concat_axis=0)
+    filled = jnp.concatenate(blocks, axis=0)
     parts = jnp.split(filled, [sum(widths[:k]) for k in range(1, len(widths))], axis=1)
     return tuple(
         (

time: 353 us -> 474 us (1.34)
  waiting for transfers between devices: 170 us -> 275 us
  starting transfers between devices: 55 us -> 63.4 us
  blocking collectives: 29.4 us -> 35.2 us
    ppermute x4, waiting for transfers between devices: 0.01 us -> 177 us  [extended(): lax.ppermute(tail, axis, [(i, (i + 1) % count) for i in range(ends)])]
    all_gather x1 -> x0, waiting for transfers between devices: 89.3 us -> none  [turned_gather(): filled = lax.all_gather(both, axis, axis=0, tiled=True)]
    ppermute x4, waiting for transfers between devices: 4.15 us -> 23.5 us  [extended(): lax.ppermute(head, axis, [((i + 1) % count, i) for i in range(ends)])]
    reshape x1 -> x2, local copies, waits for them, and re-layouts: 0.01 us -> 8.47 us  [the longest x1 8.47 us: turned_gather(): filled = jnp.concatenate(blocks, axis=0)]
    unnamed x28 -> x45, local copies, waits for them, and re-layouts: 16.4 us -> 7.98 us
    all_to_all x0 -> x1, starting transfers between devices: none -> 5.84 us  [turned_gather(): blocks = lax.all_to_all(blocks, axis, split_axis=0, concat_axis=0)]
    all_to_all x3, blocking collectives: 29.4 us -> 35.2 us  [from_everyone(): lax.all_to_all(jnp.broadcast_to(shard[None], (length, *shard.shape)), axi...]
  transfers between devices with their start and end apart: 14 -> 14, of which waited for: 8 -> 9; matrix products, arithmetic and copies ran while one was open for 6% -> 4% of each run, Pallas kernels for 0% -> 0%
where the time goes in v1:
time: 474 us; the launch traced here: 472 us
  waiting for transfers between devices  275 us (58%)
  starting transfers between devices  63.4 us (13%)
  matrix products  37.3 us (8%)
  blocking collectives  35.2 us (7%)
  local copies, waits for them, and re-layouts  33.3 us (7%)
  between operations  16.5 us (3%)
  other arithmetic  11.2 us (2%)
    ppermute x4, waiting for transfers between devices, extended(): lax.ppermute(tail, axis, [(i, (i + 1) % count) for i in range(ends)])  177 us
    all_gather x1, waiting for transfers between devices, in_one_piece(): filled = lax.all_gather(both, axis, axis=dim, tiled=True)  39.1 us
    all_to_all x3, blocking collectives, from_everyone(): lax.all_to_all(jnp.broadcast_to(shard[None], (length, *shard.shape)), axi...  35.2 us
    all_to_all x3, starting transfers between devices, from_everyone(): lax.all_to_all(jnp.broadcast_to(shard[None], (length, *shard.shape)), axi...  25.3 us
    ppermute x4, waiting for transfers between devices, extended(): lax.ppermute(head, axis, [((i + 1) % count, i) for i in range(ends)])  23.5 us
    all_to_all x3, waiting for transfers between devices, from_everyone(): lax.all_to_all(jnp.broadcast_to(shard[None], (length, *shard.shape)), axi...  22.2 us
    dot_general x36, matrix products, convolve(): jnp.einsum('bhwc,cd->bhwd', window, kernel[offset * width_in:(offset + 1)...  20.7 us
    ppermute x4, starting transfers between devices, extended(): lax.ppermute(tail, axis, [(i, (i + 1) % count) for i in range(ends)])  14.4 us
  transfers between devices with their start and end apart: 14, of which 9 were waited for; matrix products, arithmetic and copies ran while one was open for 4% of the time, Pallas kernels for 0%

profile of v1, /device:TPU:1, one launch (start us, length us, event | category | flops | bytes accessed | tf_op | source)
XLA Modules:
  0.0 471.9 jit_solution(3378530029774866280)
XLA Ops:
  10.7 4.6 collective-permute-start
  15.3 5.5 %collective-permute-start.1 = (bf16[1,1,64,4]{2,3,1,0:T(4,128)(2,1)S(1)}, bf16[1,1,64,4]{2,3,1,0:T(4,128)(2,1)S(1)}, u32[]{:S(2)}, u32[]{:S(2)}) collective-permute-start(bf16[1,1,64,4]{2,3,1,0:T(4,128)(2,1)S(1)} %get-tuple-element.38), channel_id=1, source_target_pairs={{1,0},{2,1},{3,2},{4,3},{5,4},{6,5},{7,6},{9,8},{10,9},{11,10},{12... | collective-permute-start | bytes 1544 | tf_op jit(solution)/shard_map/ppermute | solution.py:43
  21.4 14.3 %all-to-all-start.2 = ((s32[64,1,1]{2,1,0:T(1,128)}), s32[64,1,1]{2,1,0:T(1,128)S(1)}, u32[]{:S(2)}, u32[]{:S(2)}) async-start(s32[64,1,1]{2,1,0:T(1,128)} %broadcast_in_dim.22), calls=%async_computation.2 | async-start | bytes 65536 | tf_op jit(solution)/shard_map/all_to_all | solution.py:24
  37.2 11.6 %all-to-all-done.2 = s32[64,1,1]{2,1,0:T(1,128)S(1)} async-done(((s32[64,1,1]{2,1,0:T(1,128)}), s32[64,1,1]{2,1,0:T(1,128)S(1)}, u32[]{:S(2)}, u32[]{:S(2)}) %all-to-all-start.2) | async-done | bytes 288 | tf_op jit(solution)/shard_map/all_to_all | solution.py:24
  51.6 4.6 all-to-all-start.3
  62.4 7.2 %all-to-all-done.3 = bf16[64,2,640]{2,1,0:T(2,128)(2,1)S(1)} async-done(((bf16[64,2,640]{2,1,0:T(2,128)(2,1)}), bf16[64,2,640]{2,1,0:T(2,128)(2,1)S(1)}, u32[]{:S(2)}, u32[]{:S(2)}) %all-to-all-start.3) | async-done | bytes 163872 | tf_op jit(solution)/shard_map/all_to_all | solution.py:24
  70.2 6.3 %all-to-all-start = ((f32[8,1,64]{2,1,0:T(1,128)}), f32[8,1,64]{2,1,0:T(1,128)S(1)}, u32[]{:S(2)}, u32[]{:S(2)}) async-start(f32[8,1,64]{2,1,0:T(1,128)} %broadcast_in_dim.21), calls=%async_computation | async-start | bytes 8192 | tf_op jit(solution)/shard_map/all_to_all | solution.py:24
  77.9 3.4 all-to-all-done
  81.3 6.4 %all-to-all-start.4 = ((f32[64,1,5]{2,1,0:T(1,128)}), f32[64,1,5]{2,1,0:T(1,128)S(1)}, u32[]{:S(2)}, u32[]{:S(2)}) async-start(f32[64,1,5]{2,1,0:T(1,128)} %copy.45), calls=%async_computation.4 | async-start | bytes 65536 | tf_op jit(solution)/shard_map/all_to_all | solution.py:118
  88.0 12.9 %all-to-all-done.4 = f32[64,1,5]{2,1,0:T(1,128)S(1)} async-done(((f32[64,1,5]{2,1,0:T(1,128)}), f32[64,1,5]{2,1,0:T(1,128)S(1)}, u32[]{:S(2)}, u32[]{:S(2)}) %all-to-all-start.4) | async-done | bytes 1312 | tf_op jit(solution)/shard_map/all_to_all | solution.py:118
  100.9 3.7 stack.2
  104.6 5.8 %all-to-all-start.1 = ((bf16[64,5,7680]{2,1,0:T(8,128)(2,1)}), bf16[64,5,7680]{2,1,0:T(8,128)(2,1)}, u32[]{:S(2)}, u32[]{:S(2)}) async-start(bf16[64,5,7680]{2,1,0:T(8,128)(2,1)} %stack.2), calls=%async_computation.1 | async-start | bytes 15728640 | tf_op jit(solution)/shard_map/all_to_all | solution.py:77
  111.1 4.3 collective-permute-start.2
  117.5 177.2 %collective-permute-done.2 = bf16[1,1,64,320]{3,2,1,0:T(8,128)(2,1)S(1)} collective-permute-done((bf16[1,1,64,320]{3,2,1,0:T(8,128)(2,1)S(1)}, bf16[1,1,64,320]{3,2,1,0:T(8,128)(2,1)S(1)}, u32[]{:S(2)}, u32[]{:S(2)}) %collective-permute-start.2) | collective-permute-done | bytes 40992 | tf_op jit(solution)/shard_map/ppermute | solution.py:41
  294.7 19.2 %collective-permute-done.3 = bf16[1,1,64,320]{3,2,1,0:T(8,128)(2,1)S(1)} collective-permute-done((bf16[1,1,64,320]{3,2,1,0:T(8,128)(2,1)S(1)}, bf16[1,1,64,320]{3,2,1,0:T(8,128)(2,1)S(1)}, u32[]{:S(2)}, u32[]{:S(2)}) %collective-permute-start.3) | collective-permute-done | bytes 40992 | tf_op jit(solution)/shard_map/ppermute | solution.py:43
  315.4 8.5 %reshape.834 = bf16[320,7680]{1,0:T(8,128)(2,1)} reshape(bf16[64,5,7680]{2,1,0:T(8,128)(2,1)} %all-to-all-done.1) | data formatting | bytes 9830400 | tf_op jit(solution)/shard_map/reshape | solution.py:78
  323.9 4.3 fusion.187
  328.2 4.0 copy.51
  339.1 19.6 %all_to_all.53 = f32[8,1,64]{2,1,0:T(1,128)S(1)} all-to-all(f32[8,1,64]{2,1,0:T(1,128)S(1)} %broadcast_in_dim.24), channel_id=1, replica_groups=mesh['batch'=64,'space'=8] {'space'}, dimensions={0} | all-to-all | bytes 4096 | tf_op jit(solution)/shard_map/all_to_all | solution.py:24
  359.4 2.8 collective-permute-start.4
  374.6 7.4 %all_to_all.54 = f32[8,1,64]{2,1,0:T(1,128)S(1)} all-to-all(f32[8,1,64]{2,1,0:T(1,128)S(1)} %broadcast_in_dim.26), channel_id=1, replica_groups=mesh['batch'=64,'space'=8] {'space'}, dimensions={0} | all-to-all | bytes 4096 | tf_op jit(solution)/shard_map/all_to_all | solution.py:24
  388.4 39.1 %all-gather.2.cloned.1.call-done = bf16[2,2048,320]{1,2,0:T(8,128)(2,1)} async-done(((bf16[2,256,320]{1,2,0:T(8,128)(2,1)}), bf16[2,2048,320]{1,2,0:T(8,128)(2,1)}) %all-gather.2.cloned.1.call-update) | async-done | bytes 2621456 | tf_op jit(solution)/shard_map/all_gather | solution.py:67
  445.2 8.2 %all_to_all.55 = f32[8,1,64]{2,1,0:T(1,128)S(1)} all-to-all(f32[8,1,64]{2,1,0:T(1,128)S(1)} %broadcast_in_dim.28), channel_id=1, replica_groups=mesh['batch'=64,'space'=8] {'space'}, dimensions={0} | all-to-all | bytes 4096 | tf_op jit(solution)/shard_map/all_to_all | solution.py:24
  458.8 3.5 collective-permute-done.7
  (201 shorter events, 71.1 us)
Async XLA Ops:
  6.5 70.5 %copy-start = (bf16[1280,5]{0,1:T(8,128)(2,1)S(1)}, bf16[1280,5]{0,1:T(8,128)(2,1)}, u32[]{:S(2)}) copy-start(bf16[1280,5]{0,1:T(8,128)(2,1)} %param.28) | copy-start | bytes 38404
  6.5 53.9 %copy-start.4 = (bf16[36,320]{1,0:T(8,128)(2,1)S(1)}, bf16[36,320]{1,0:T(8,128)(2,1)}, u32[]{:S(2)}) copy-start(bf16[36,320]{1,0:T(8,128)(2,1)} %param.25) | copy-start | bytes 69124
  10.7 45.6 %collective-permute-start = (bf16[1,1,64,4]{2,3,1,0:T(4,128)(2,1)S(1)}, bf16[1,1,64,4]{2,3,1,0:T(4,128)(2,1)S(1)}, u32[]{:S(2)}, u32[]{:S(2)}) collective-permute-start(bf16[1,1,64,4]{2,3,1,0:T(4,128)(2,1)S(1)} %get-tuple-element.37), channel_id=1, source_target_pairs={{0,1},{1,2},{2,3},{3,4},{4,5},{5,6},{6,7},{8,9},{9,10},{10,11},{11... | collective-permute-start | bytes 1544 | tf_op jit(solution)/shard_map/ppermute | solution.py:41
  15.3 41.0 %collective-permute-start.1 = (bf16[1,1,64,4]{2,3,1,0:T(4,128)(2,1)S(1)}, bf16[1,1,64,4]{2,3,1,0:T(4,128)(2,1)S(1)}, u32[]{:S(2)}, u32[]{:S(2)}) collective-permute-start(bf16[1,1,64,4]{2,3,1,0:T(4,128)(2,1)S(1)} %get-tuple-element.38), channel_id=1, source_target_pairs={{1,0},{2,1},{3,2},{4,3},{5,4},{6,5},{7,6},{9,8},{10,9},{11,10},{12... | collective-permute-start | bytes 1544 | tf_op jit(solution)/shard_map/ppermute | solution.py:43
  21.4 27.5 %all-to-all-start.2 = ((s32[64,1,1]{2,1,0:T(1,128)}), s32[64,1,1]{2,1,0:T(1,128)S(1)}, u32[]{:S(2)}, u32[]{:S(2)}) async-start(s32[64,1,1]{2,1,0:T(1,128)} %broadcast_in_dim.22), calls=%async_computation.2 | async-start | bytes 65536 | tf_op jit(solution)/shard_map/all_to_all | solution.py:24
  51.6 18.0 %all-to-all-start.3 = ((bf16[64,2,640]{2,1,0:T(2,128)(2,1)}), bf16[64,2,640]{2,1,0:T(2,128)(2,1)S(1)}, u32[]{:S(2)}, u32[]{:S(2)}) async-start(bf16[64,2,640]{2,1,0:T(2,128)(2,1)} %reshape.916), calls=%async_computation.3 | async-start | bytes 327680 | tf_op jit(solution)/shard_map/all_to_all | solution.py:24
  58.3 29.4 %copy-start.5 = (bf16[2880,5]{0,1:T(8,128)(2,1)S(1)}, bf16[2880,5]{0,1:T(8,128)(2,1)}, u32[]{:S(2)}) copy-start(bf16[2880,5]{0,1:T(8,128)(2,1)} %param.30) | copy-start | bytes 86404
  58.3 29.4 %copy-start.6 = (bf16[2880,5]{0,1:T(8,128)(2,1)S(1)}, bf16[2880,5]{0,1:T(8,128)(2,1)}, u32[]{:S(2)}) copy-start(bf16[2880,5]{0,1:T(8,128)(2,1)} %param.31) | copy-start | bytes 86404
  58.4 29.4 %copy-start.8 = (bf16[320,5]{0,1:T(8,128)(2,1)S(1)}, bf16[320,5]{0,1:T(8,128)(2,1)}, u32[]{:S(2)}) copy-start(bf16[320,5]{0,1:T(8,128)(2,1)} %param.32) | copy-start | bytes 9604
  58.4 29.4 %copy-start.9 = (bf16[320,5]{0,1:T(8,128)(2,1)S(1)}, bf16[320,5]{0,1:T(8,128)(2,1)}, u32[]{:S(2)}) copy-start(bf16[320,5]{0,1:T(8,128)(2,1)} %param.33) | copy-start | bytes 9604
  58.4 29.4 %copy-start.10 = (bf16[320,5]{0,1:T(8,128)(2,1)S(1)}, bf16[320,5]{0,1:T(8,128)(2,1)}, u32[]{:S(2)}) copy-start(bf16[320,5]{0,1:T(8,128)(2,1)} %param.34) | copy-start | bytes 9604
  58.4 29.4 %copy-start.11 = (bf16[320,5]{0,1:T(8,128)(2,1)S(1)}, bf16[320,5]{0,1:T(8,128)(2,1)}, u32[]{:S(2)}) copy-start(bf16[320,5]{0,1:T(8,128)(2,1)} %param.35) | copy-start | bytes 9604
  58.4 29.4 %copy-start.12 = (bf16[320,5]{0,1:T(8,128)(2,1)S(1)}, bf16[320,5]{0,1:T(8,128)(2,1)}, u32[]{:S(2)}) copy-start(bf16[320,5]{0,1:T(8,128)(2,1)} %param.36) | copy-start | bytes 9604
  58.4 29.4 %copy-start.13 = (bf16[320,5]{0,1:T(8,128)(2,1)S(1)}, bf16[320,5]{0,1:T(8,128)(2,1)}, u32[]{:S(2)}) copy-start(bf16[320,5]{0,1:T(8,128)(2,1)} %param.37) | copy-start | bytes 9604
  70.2 11.1 %all-to-all-start = ((f32[8,1,64]{2,1,0:T(1,128)}), f32[8,1,64]{2,1,0:T(1,128)S(1)}, u32[]{:S(2)}, u32[]{:S(2)}) async-start(f32[8,1,64]{2,1,0:T(1,128)} %broadcast_in_dim.21), calls=%async_computation | async-start | bytes 8192 | tf_op jit(solution)/shard_map/all_to_all | solution.py:24
  81.3 19.6 %all-to-all-start.4 = ((f32[64,1,5]{2,1,0:T(1,128)}), f32[64,1,5]{2,1,0:T(1,128)S(1)}, u32[]{:S(2)}, u32[]{:S(2)}) async-start(f32[64,1,5]{2,1,0:T(1,128)} %copy.45), calls=%async_computation.4 | async-start | bytes 65536 | tf_op jit(solution)/shard_map/all_to_all | solution.py:118
  104.6 210.8 %all-to-all-start.1 = ((bf16[64,5,7680]{2,1,0:T(8,128)(2,1)}), bf16[64,5,7680]{2,1,0:T(8,128)(2,1)}, u32[]{:S(2)}, u32[]{:S(2)}) async-start(bf16[64,5,7680]{2,1,0:T(8,128)(2,1)} %stack.2), calls=%async_computation.1 | async-start | bytes 15728640 | tf_op jit(solution)/shard_map/all_to_all | solution.py:77
  110.4 317.1 %all-gather.2.cloned.1.call-start = ((), (), s32[]{:S(2)}) async-start(), calls=%async_computation.8 | async-start | bytes 2949120 | tf_op jit(solution)/shard_map/all_gather | solution.py:67
  111.1 183.6 %collective-permute-start.2 = (bf16[1,1,64,320]{3,2,1,0:T(8,128)(2,1)S(1)}, bf16[1,1,64,320]{3,2,1,0:T(8,128)(2,1)S(1)}, u32[]{:S(2)}, u32[]{:S(2)}) collective-permute-start(bf16[1,1,64,320]{3,2,1,0:T(8,128)(2,1)S(1)} %get-tuple-element.34), channel_id=1, source_target_pairs={{0,1},{1,2},{2,3},{3,4},{4,5},{5,6},{6,7},{8,9},{9,10},{10,11},{11... | collective-permute-start | bytes 122888 | tf_op jit(solution)/shard_map/ppermute | solution.py:41
  115.4 198.5 %collective-permute-start.3 = (bf16[1,1,64,320]{3,2,1,0:T(8,128)(2,1)S(1)}, bf16[1,1,64,320]{3,2,1,0:T(8,128)(2,1)S(1)}, u32[]{:S(2)}, u32[]{:S(2)}) collective-permute-start(bf16[1,1,64,320]{3,2,1,0:T(8,128)(2,1)S(1)} %get-tuple-element.35), channel_id=1, source_target_pairs={{1,0},{2,1},{3,2},{4,3},{5,4},{6,5},{7,6},{9,8},{10,9},{11,10},{12... | collective-permute-start | bytes 122888 | tf_op jit(solution)/shard_map/ppermute | solution.py:43
  359.4 7.3 %collective-permute-start.4 = (bf16[1,1,64,320]{3,2,1,0:T(8,128)(2,1)S(1)}, bf16[1,1,64,320]{3,2,1,0:T(8,128)(2,1)S(1)}, u32[]{:S(2)}, u32[]{:S(2)}) collective-permute-start(bf16[1,1,64,320]{3,2,1,0:T(8,128)(2,1)S(1)} %get-tuple-element.32), channel_id=1, source_target_pairs={{0,1},{1,2},{2,3},{3,4},{4,5},{5,6},{6,7},{8,9},{9,10},{10,11},{11... | collective-permute-start | bytes 122888 | tf_op jit(solution)/shard_map/ppermute | solution.py:41
  362.2 5.4 %collective-permute-start.5 = (bf16[1,1,64,320]{3,2,1,0:T(8,128)(2,1)S(1)}, bf16[1,1,64,320]{3,2,1,0:T(8,128)(2,1)S(1)}, u32[]{:S(2)}, u32[]{:S(2)}) collective-permute-start(bf16[1,1,64,320]{3,2,1,0:T(8,128)(2,1)S(1)} %get-tuple-element.33), channel_id=1, source_target_pairs={{1,0},{2,1},{3,2},{4,3},{5,4},{6,5},{7,6},{9,8},{10,9},{11,10},{12... | collective-permute-start | bytes 122888 | tf_op jit(solution)/shard_map/ppermute | solution.py:43
  454.0 4.7 %collective-permute-start.6 = (bf16[1,1,64,320]{3,2,1,0:T(8,128)(2,1)S(1)}, bf16[1,1,64,320]{3,2,1,0:T(8,128)(2,1)S(1)}, u32[]{:S(2)}, u32[]{:S(2)}) collective-permute-start(bf16[1,1,64,320]{3,2,1,0:T(8,128)(2,1)S(1)} %get-tuple-element.30), channel_id=1, source_target_pairs={{0,1},{1,2},{2,3},{3,4},{4,5},{5,6},{6,7},{8,9},{9,10},{10,11},{11... | collective-permute-start | bytes 122888 | tf_op jit(solution)/shard_map/ppermute | solution.py:41
  456.8 5.4 %collective-permute-start.7 = (bf16[1,1,64,320]{3,2,1,0:T(8,128)(2,1)S(1)}, bf16[1,1,64,320]{3,2,1,0:T(8,128)(2,1)S(1)}, u32[]{:S(2)}, u32[]{:S(2)}) collective-permute-start(bf16[1,1,64,320]{3,2,1,0:T(8,128)(2,1)S(1)} %get-tuple-element.31), channel_id=1, source_target_pairs={{1,0},{2,1},{3,2},{4,3},{5,4},{6,5},{7,6},{9,8},{10,9},{11,10},{12... | collective-permute-start | bytes 122888 | tf_op jit(solution)/shard_map/ppermute | solution.py:43
  (10 other events, 139.9 us)
Sparse Core Ops, SparseCore 0:
  387.3 40.2 all-gather.1
